TPU v7x, 256 devices: a whole 4x4x8 slice. The times are simulated.
256 devices in a mesh: gz: 64 (over z, x, core), gy: 4 (over y).
Axes of the slice: x: 4, y: 4, z: 8, core: 2. Of those that a mesh axis runs over, the one named last changes fastest.
Arguments:
- iterate: float32 [128, 256, 1024], P('gz', 'gy'), may hold values from -1.5 to 1.5
- basis: bfloat16 [32, 128, 256, 1024], P(None, 'gz', 'gy'), may hold values from -6 to 6
- coeffs: float32 [32], replicated, may hold values from -0.3125 to 0.3125
- rhs: float32 [128, 256, 1024], P('gz', 'gy'), may hold values from -8 to 8
- kappa: float32 [128, 256, 1024], P('gz', 'gy'), may hold values from 0.5 to 4
- offsets: int32 [128, 256, 8], P('gz', 'gy'), may hold values from 0 to 2047
- flips: int32 [128, 256, 8], P('gz', 'gy'), may hold values from 0 to 1
Outputs:
- new_iterate: float32 [128, 256, 1024], P('gz', 'gy')
- residual: float32 [128, 256, 1024], P('gz', 'gy')
- sketch_unit: float32 [2048], replicated
All inputs are finite; a program needn't handle non-finite values.
Results may differ from a plain program's by a relative error of at most 0.00058.
Values sent between devices are 32-bit elements; how exact they have to be, the bound alone decides.
No kernel may reach another device: no remote copies, remote signals or barrier semaphores. Data moves between devices by JAX's collectives and lax.ppermute only.
A program may use at most 64 MiB of HBM per device.

v0:
```python
import jax
import jax.numpy as jnp
from jax import lax
from jax.sharding import Mesh
from jax.sharding import PartitionSpec as P

SK = 2048
BLK = 128
GZ_GY = ("gz_0", "gz_1", "gz_2", "gy")
GZ = ("gz_0", "gz_1", "gz_2")


def extended(value, sides, width):
    edges = {}
    for axis, dim in sides:
        peers, length = (lax.axis_size(axis), value.shape[dim])
        up = [(i, (i + 1) % peers) for i in range(peers - 1)]
        last = lax.slice_in_dim(value, length - width, length, axis=dim)
        initial = lax.slice_in_dim(value, 0, width, axis=dim)
        edges[dim] = (
            lax.ppermute(last, axis, up),
            lax.ppermute(initial, axis, [(b, a) for a, b in up]),
        )
    done = []
    for _, dim in sides:
        low, high = edges[dim]
        around = [(width, width) if d in done else (0, 0) for d in range(value.ndim)]
        value = jnp.concatenate([jnp.pad(low, around), value, jnp.pad(high, around)], axis=dim)
        done.append(dim)
    return value


def one_axis_at_a_time(value, axes):
    for axis in axes:
        value = lax.psum(value, axis)
    return value


def apply_operator(upad, kpad):
    field = upad[1:-1, 1:-1, :]
    coef = kpad[1:-1, 1:-1, :]
    total = 0.05 * field
    neighbours = [
        (upad[2:, 1:-1, :], kpad[2:, 1:-1, :]),
        (upad[:-2, 1:-1, :], kpad[:-2, 1:-1, :]),
        (upad[1:-1, 2:, :], kpad[1:-1, 2:, :]),
        (upad[1:-1, :-2, :], kpad[1:-1, :-2, :]),
    ]
    zero_col = jnp.zeros_like(field[:, :, :1])
    neighbours.append(
        (
            jnp.concatenate([field[:, :, 1:], zero_col], 2),
            jnp.concatenate([coef[:, :, 1:], zero_col], 2),
        )
    )
    neighbours.append(
        (
            jnp.concatenate([zero_col, field[:, :, :-1]], 2),
            jnp.concatenate([zero_col, coef[:, :, :-1]], 2),
        )
    )
    for other, kother in neighbours:
        total = total + 0.5 * (coef + kother) * (field - other)
    return total


def local_sketch(residual, offsets, flips):
    blocks = residual.reshape(-1, BLK)
    signs = (2 * flips - 1).astype(jnp.float32).reshape(-1, 1)
    columns = lax.broadcasted_iota(jnp.int32, (1, SK), 1)
    placed = jnp.where(offsets.reshape(-1, 1) == columns, signs, 0.0)
    spread = jnp.dot(
        blocks.T, placed, precision=lax.Precision.HIGHEST, preferred_element_type=jnp.float32
    )
    doubled = jnp.concatenate([spread, spread], 1).reshape(-1)
    doubled = jnp.concatenate([doubled, jnp.zeros((SK,), jnp.float32)])
    skewed = doubled[SK : SK + BLK * (2 * SK - 1)].reshape(BLK, 2 * SK - 1)
    return jnp.sum(skewed[:, :SK], axis=0)


def shards(iterate, basis, coeffs, rhs, kappa, offsets, flips):
    coeff_b = coeffs.astype(jnp.bfloat16)
    new_iterate = iterate + jnp.einsum(
        "k,kzyx->zyx", coeff_b, basis, preferred_element_type=jnp.float32
    )
    stacked = jnp.stack([new_iterate, kappa])
    padded = extended(stacked, ((GZ, 1), ("gy", 2)), 1)
    upad = padded[0]
    kpad = padded[1]
    residual = rhs - apply_operator(upad, kpad)
    partial_sketch = local_sketch(residual, offsets, flips)
    sketch = one_axis_at_a_time(partial_sketch, GZ_GY)
    sketch_unit = sketch / jnp.sqrt(jnp.mean(sketch * sketch) + 1e-06)
    return (new_iterate, residual, sketch_unit)


def solution(mesh):
    finer = Mesh(mesh.devices.reshape(8, 4, 2, mesh.shape["gy"]), ("gz_0", "gz_1", "gz_2", "gy"))
    placed = (
        P(GZ, "gy", None),
        P(None, GZ, "gy", None),
        P(),
        P(GZ, "gy", None),
        P(GZ, "gy", None),
        P(GZ, "gy", None),
        P(GZ, "gy", None),
    )
    return jax.shard_map(
        shards,
        mesh=finer,
        in_specs=placed,
        out_specs=(P(GZ, "gy", None), P(GZ, "gy", None), P()),
        check_vma=False,
    )
```

profile of v0, /device:TPU:2, one launch (start us, length us, event | category | flops | bytes accessed | tf_op | source)
XLA Modules:
  0.0 85.2 jit_solution(9888327381164182605)
XLA Ops:
  0.6 0.0 copy-start.3
  0.6 0.0 copy-start.1
  0.7 12.6 %fusion = f32[1,2,64,1024]{3,0,2,1:T(1,128)S(1)} fusion(bf16[32,2,64,1024]{3,2,1,0:T(8,128)(2,1)} %param.8, f32[32]{0:T(128)} %param.9), kind=kOutput, calls=%fused_computation | convolution fusion | flops 8388640 | bytes 8913024 | tf_op jit(solution)/shard_map/k,kzyx->zyx/dot_general | solution.py:83
  13.2 0.0 copy-done.3
  13.2 0.0 copy-start.6
  13.2 0.0 copy-start.5
  13.2 0.1 bitcast_add_fusion
  13.4 0.0 copy-start
  13.4 0.0 copy-done.1
  13.4 0.1 fusion.8
  13.5 1.9 %collective-permute-start.1 = (f32[2,1,64,1024]{3,2,1,0:T(8,128)S(1)}, f32[2,1,64,1024]{3,2,1,0:T(8,128)S(1)}, u32[]{:S(2)}, u32[]{:S(2)}) collective-permute-start(f32[2,1,64,1024]{3,2,1,0:T(8,128)S(1)} %get-tuple-element.9), channel_id=1, source_target_pairs={{0,4},{4,8},{8,12},{12,16},{16,20},{20,24},{24,28},{28,32},{32,36}... | collective-permute-start | bytes 1572872 | tf_op jit(solution)/shard_map/ppermute | solution.py:21
  15.4 3.6 %collective-permute-start.2 = (f32[2,1,64,1024]{3,2,1,0:T(8,128)S(1)}, f32[2,1,64,1024]{3,2,1,0:T(8,128)S(1)}, u32[]{:S(2)}, u32[]{:S(2)}) collective-permute-start(f32[2,1,64,1024]{3,2,1,0:T(8,128)S(1)} %get-tuple-element.10), channel_id=1, source_target_pairs={{4,0},{8,4},{12,8},{16,12},{20,16},{24,20},{28,24},{32,28},{36,32}... | collective-permute-start | bytes 1572872 | tf_op jit(solution)/shard_map/ppermute | solution.py:22
  19.1 3.5 %collective-permute-start = (f32[2,2,1,1024]{3,2,1,0:T(1,128)S(1)}, f32[2,2,1,1024]{3,2,1,0:T(1,128)S(1)}, u32[]{:S(2)}, u32[]{:S(2)}) collective-permute-start(f32[2,2,1,1024]{3,2,1,0:T(1,128)S(1)} %get-tuple-element.11), channel_id=1, source_target_pairs={{0,1},{1,2},{2,3},{4,5},{5,6},{6,7},{8,9},{9,10},{10,11},{12,13},{... | collective-permute-start | bytes 49160 | tf_op jit(solution)/shard_map/ppermute | solution.py:21
  22.6 1.5 %collective-permute-start.3 = (f32[2,2,1,1024]{3,2,1,0:T(1,128)S(1)}, f32[2,2,1,1024]{3,2,1,0:T(1,128)S(1)}, u32[]{:S(2)}, u32[]{:S(2)}) collective-permute-start(f32[2,2,1,1024]{3,2,1,0:T(1,128)S(1)} %get-tuple-element.12), channel_id=1, source_target_pairs={{1,0},{2,1},{3,2},{5,4},{6,5},{7,6},{9,8},{10,9},{11,10},{13,12},{... | collective-permute-start | bytes 49160 | tf_op jit(solution)/shard_map/ppermute | solution.py:22
  24.1 0.0 copy-done.6
  24.1 0.1 copy.13
  24.2 0.1 broadcast_in_dim.16
  24.3 0.0 copy-done.5
  24.3 0.1 copy.12
  24.4 0.1 eq.15
  24.5 0.0 collective-permute-done
  24.5 3.7 %collective-permute-done.3 = f32[2,2,1,1024]{3,2,1,0:T(1,128)S(1)} collective-permute-done((f32[2,2,1,1024]{3,2,1,0:T(1,128)S(1)}, f32[2,2,1,1024]{3,2,1,0:T(1,128)S(1)}, u32[]{:S(2)}, u32[]{:S(2)}) %collective-permute-start.3) | collective-permute-done | bytes 16416 | tf_op jit(solution)/shard_map/ppermute | solution.py:22
  28.2 0.0 collective-permute-done.1
  28.2 0.0 collective-permute-done.2
  28.2 0.3 select_maximum_fusion
  28.6 0.0 copy-done
  28.6 0.2 slice_bitcast_fusion
  28.7 0.0 copy-start.4
  28.7 0.5 fusion.27
  29.2 0.6 copy-done.4
  29.8 0.8 fusion.13
  30.6 0.0 copy-start.2
  30.6 0.1 reshape.19
  30.7 5.4 %fusion.2 = f32[128,2048]{1,0:T(8,128)S(1)} fusion(f32[1024,128]{1,0:T(8,128)S(1)} %reshape.19, f32[1024]{0:T(1024)S(1)} %broadcast_in_dim.16, s32[1024]{0:T(1024)S(1)} %eq.15), kind=kOutput, calls=%fused_computation.2 | convolution fusion | flops 3225419776 | bytes 1581056 | tf_op jit(solution)/shard_map/dot_general | solution.py:72
  36.1 0.0 copy-done.2
  36.1 0.2 maximum_bitcast_fusion
  36.4 0.4 copy.17
  36.8 0.1 pad_slice_fusion
  36.9 2.5 %reshape.21 = f32[128,4095]{1,0:T(8,128)} reshape(f32[524160]{0:T(1024)S(1)} %pad_slice_fusion) | data formatting | bytes 4193280 | tf_op jit(solution)/shard_map/reshape | solution.py:77
  39.4 1.3 %slice_reduce_fusion = f32[2048]{0:T(1024)S(1)} fusion(f32[128,4095]{1,0:T(8,128)} %reshape.21), kind=kLoop, calls=%fused_computation.20 | loop fusion | flops 260096 | bytes 1056768 | tf_op jit(solution)/shard_map/reduce_sum | solution.py:78
  40.7 20.3 %psum.28 = f32[2048]{0:T(1024)S(1)} all-reduce(f32[2048]{0:T(1024)S(1)} %slice_reduce_fusion), channel_id=1, replica_groups=mesh['gz_0'=8,'gz_1'=4,'gz_2'=2,'gy'=4] {'gz_0'}, use_global_device_ids=true, to_apply=%region_1.2 | all-reduce | flops 2048 | bytes 16384 | tf_op jit(solution)/shard_map/psum | solution.py:35
  60.9 10.5 %psum.29 = f32[2048]{0:T(1024)S(1)} all-reduce(f32[2048]{0:T(1024)S(1)} %psum.28), channel_id=1, replica_groups=mesh['gz_0'=8,'gz_1'=4,'gz_2'=2,'gy'=4] {'gz_1'}, use_global_device_ids=true, to_apply=%region_2.3 | all-reduce | flops 2048 | bytes 16384 | tf_op jit(solution)/shard_map/psum | solution.py:35
  71.4 2.5 %psum.30 = f32[2048]{0:T(1024)S(1)} all-reduce(f32[2048]{0:T(1024)S(1)} %psum.29), channel_id=1, replica_groups=mesh['gz_0'=8,'gz_1'=4,'gz_2'=2,'gy'=4] {'gz_2'}, use_global_device_ids=true, to_apply=%region_3.4 | all-reduce | flops 2048 | bytes 16384 | tf_op jit(solution)/shard_map/psum | solution.py:35
  73.9 9.4 %psum.31 = f32[2048]{0:T(1024)S(1)} all-reduce(f32[2048]{0:T(1024)S(1)} %psum.30), channel_id=1, replica_groups=mesh['gz_0'=8,'gz_1'=4,'gz_2'=2,'gy'=4] {'gy'}, use_global_device_ids=true, to_apply=%region_4.5 | all-reduce | flops 2048 | bytes 16384 | tf_op jit(solution)/shard_map/psum | solution.py:35
  83.3 0.6 multiply_reduce_fusion
  84.6 0.6 broadcast_divide_fusion
  (2 shorter events, 0.0 us)
Async XLA Ops:
  0.6 12.6 %copy-start.3 = (f32[2,64,1024]{2,1,0:T(8,128)S(1)}, f32[2,64,1024]{2,1,0:T(8,128)}, u32[]{:S(2)}) copy-start(f32[2,64,1024]{2,1,0:T(8,128)} %param.7) | copy-start | bytes 1572868
  0.6 12.7 %copy-start.1 = (f32[2,64,1024]{2,1,0:T(8,128)S(1)}, f32[2,64,1024]{2,1,0:T(8,128)}, u32[]{:S(2)}) copy-start(f32[2,64,1024]{2,1,0:T(8,128)} %param.11) | copy-start | bytes 1572868
  13.2 10.9 %copy-start.6 = (s32[2,64,8]{1,2,0:T(8,128)S(1)}, s32[2,64,8]{1,2,0:T(8,128)}, u32[]{:S(2)}) copy-start(s32[2,64,8]{1,2,0:T(8,128)} %param.13) | copy-start | bytes 12292
  13.2 11.1 %copy-start.5 = (s32[2,64,8]{1,2,0:T(8,128)S(1)}, s32[2,64,8]{1,2,0:T(8,128)}, u32[]{:S(2)}) copy-start(s32[2,64,8]{1,2,0:T(8,128)} %param.12) | copy-start | bytes 12292
  13.4 15.2 %copy-start = (f32[2,64,1024]{2,1,0:T(8,128)}, f32[2,64,1024]{2,1,0:T(8,128)S(1)}, u32[]{:S(2)}) copy-start(f32[2,64,1024]{2,1,0:T(8,128)S(1)} %bitcast_add_fusion) | copy-start | bytes 1572868
  13.5 14.7 %collective-permute-start.1 = (f32[2,1,64,1024]{3,2,1,0:T(8,128)S(1)}, f32[2,1,64,1024]{3,2,1,0:T(8,128)S(1)}, u32[]{:S(2)}, u32[]{:S(2)}) collective-permute-start(f32[2,1,64,1024]{3,2,1,0:T(8,128)S(1)} %get-tuple-element.9), channel_id=1, source_target_pairs={{0,4},{4,8},{8,12},{12,16},{16,20},{20,24},{24,28},{28,32},{32,36}... | collective-permute-start | bytes 1572872 | tf_op jit(solution)/shard_map/ppermute | solution.py:21
  15.4 12.8 %collective-permute-start.2 = (f32[2,1,64,1024]{3,2,1,0:T(8,128)S(1)}, f32[2,1,64,1024]{3,2,1,0:T(8,128)S(1)}, u32[]{:S(2)}, u32[]{:S(2)}) collective-permute-start(f32[2,1,64,1024]{3,2,1,0:T(8,128)S(1)} %get-tuple-element.10), channel_id=1, source_target_pairs={{4,0},{8,4},{12,8},{16,12},{20,16},{24,20},{28,24},{32,28},{36,32}... | collective-permute-start | bytes 1572872 | tf_op jit(solution)/shard_map/ppermute | solution.py:22
  19.1 5.4 %collective-permute-start = (f32[2,2,1,1024]{3,2,1,0:T(1,128)S(1)}, f32[2,2,1,1024]{3,2,1,0:T(1,128)S(1)}, u32[]{:S(2)}, u32[]{:S(2)}) collective-permute-start(f32[2,2,1,1024]{3,2,1,0:T(1,128)S(1)} %get-tuple-element.11), channel_id=1, source_target_pairs={{0,1},{1,2},{2,3},{4,5},{5,6},{6,7},{8,9},{9,10},{10,11},{12,13},{... | collective-permute-start | bytes 49160 | tf_op jit(solution)/shard_map/ppermute | solution.py:21
  22.6 5.6 %collective-permute-start.3 = (f32[2,2,1,1024]{3,2,1,0:T(1,128)S(1)}, f32[2,2,1,1024]{3,2,1,0:T(1,128)S(1)}, u32[]{:S(2)}, u32[]{:S(2)}) collective-permute-start(f32[2,2,1,1024]{3,2,1,0:T(1,128)S(1)} %get-tuple-element.12), channel_id=1, source_target_pairs={{1,0},{2,1},{3,2},{5,4},{6,5},{7,6},{9,8},{10,9},{11,10},{13,12},{... | collective-permute-start | bytes 49160 | tf_op jit(solution)/shard_map/ppermute | solution.py:22
  28.7 1.0 %copy-start.4 = (f32[2,64,1024]{2,1,0:T(8,128)S(1)}, f32[2,64,1024]{2,1,0:T(8,128)}, u32[]{:S(2)}) copy-start(f32[2,64,1024]{2,1,0:T(8,128)} %param.10) | copy-start | bytes 1572868
  30.6 5.6 %copy-start.2 = (f32[2,64,1024]{2,1,0:T(8,128)}, f32[2,64,1024]{2,1,0:T(8,128)S(1)}, u32[]{:S(2)}) copy-start(f32[2,64,1024]{2,1,0:T(8,128)S(1)} %fusion.13) | copy-start | bytes 1572868
where the time goes:
time: 85.6 us; the launch traced here: 85.2 us
  blocking collectives  42.6 us (50%)
  matrix products  18 us (21%)
  starting transfers between devices  10.5 us (12%)
  local copies, waits for them, and re-layouts  4.64 us (5%)
  other arithmetic  4.1 us (5%)
  waiting for transfers between devices  3.73 us (4%)
  between operations  1.59 us (2%)
    psum x4, blocking collectives, one_axis_at_a_time(): value = lax.psum(value, axis)  42.6 us
    dot_general x1, matrix products, shards(): jnp.einsum('k,kzyx->zyx', coeff_b, basis, preferred_element_type=jnp.floa...  12.6 us
    dot_general x1, matrix products, local_sketch(): jnp.dot(blocks.T, placed, precision=lax.Precision.HIGHEST, preferred_elem...  5.44 us
    ppermute x2, starting transfers between devices, extended(): lax.ppermute(last, axis, up)  5.4 us
    ppermute x2, starting transfers between devices, extended(): lax.ppermute(initial, axis, [(b, a) for a, b in up])  5.11 us
    ppermute x2, waiting for transfers between devices, extended(): lax.ppermute(initial, axis, [(b, a) for a, b in up])  3.72 us
    reshape x1, local copies, waits for them, and re-layouts, local_sketch(): skewed = doubled[SK:SK + BLK * (2 * SK - 1)].reshape(BLK, 2 * SK - 1)  2.47 us
  transfers between devices with their start and end apart: 4, of which 1 were waited for; matrix products, arithmetic and copies ran while one was open for 0% of the time, Pallas kernels for 0%

commit v1 on v0

--- a/solution.py
+++ b/solution.py
@@ -32,7 +32,7 @@
 
 def one_axis_at_a_time(value, axes):
     for axis in axes:
-        value = lax.psum(value, axis)
+        value = jnp.sum(lax.all_gather(value, axis), axis=0)
     return value
 
 

time: 85.6 us -> 98.7 us (1.15); the launches traced: 85.2 us -> 96.9 us
  blocking collectives: 42.6 us -> 54.2 us
    all_gather x0 -> x4, blocking collectives: none -> 54.2 us  [one_axis_at_a_time(): value = jnp.sum(lax.all_gather(value, axis), axis=0)]
    psum x4 -> x0, blocking collectives: 42.6 us -> none  [one_axis_at_a_time(): value = lax.psum(value, axis)]
where the time goes in v1:
time: 98.7 us; the launch traced here: 96.9 us
  blocking collectives  54.2 us (55%)
  matrix products  18 us (18%)
  starting transfers between devices  10.5 us (11%)
  local copies, waits for them, and re-layouts  4.7 us (5%)
  other arithmetic  4.2 us (4%)
  waiting for transfers between devices  3.73 us (4%)
  between operations  1.6 us (2%)
    all_gather x4, blocking collectives, one_axis_at_a_time(): value = jnp.sum(lax.all_gather(value, axis), axis=0)  54.2 us
    dot_general x1, matrix products, shards(): jnp.einsum('k,kzyx->zyx', coeff_b, basis, preferred_element_type=jnp.floa...  12.6 us
    dot_general x1, matrix products, local_sketch(): jnp.dot(blocks.T, placed, precision=lax.Precision.HIGHEST, preferred_elem...  5.44 us
    ppermute x2, starting transfers between devices, extended(): lax.ppermute(last, axis, up)  5.4 us
    ppermute x2, starting transfers between devices, extended(): lax.ppermute(initial, axis, [(b, a) for a, b in up])  5.11 us
    ppermute x2, waiting for transfers between devices, extended(): lax.ppermute(initial, axis, [(b, a) for a, b in up])  3.72 us
    reshape x1, local copies, waits for them, and re-layouts, local_sketch(): skewed = doubled[SK:SK + BLK * (2 * SK - 1)].reshape(BLK, 2 * SK - 1)  2.47 us
  transfers between devices with their start and end apart: 4, of which 1 were waited for; matrix products, arithmetic and copies ran while one was open for 0% of the time, Pallas kernels for 0%

profile of v1, /device:TPU:2, one launch (start us, length us, event | category | flops | bytes accessed | tf_op | source)
XLA Modules:
  0.0 96.9 jit_solution(7790009449335395018)
XLA Ops:
  0.6 0.0 copy-start.3
  0.6 0.0 copy-start.1
  0.7 12.6 %fusion = f32[1,2,64,1024]{3,0,2,1:T(1,128)S(1)} fusion(bf16[32,2,64,1024]{3,2,1,0:T(8,128)(2,1)} %param.8, f32[32]{0:T(128)} %param.9), kind=kOutput, calls=%fused_computation | convolution fusion | flops 8388640 | bytes 8913024 | tf_op jit(solution)/shard_map/k,kzyx->zyx/dot_general | solution.py:83
  13.2 0.0 copy-done.3
  13.2 0.0 copy-start.6
  13.2 0.0 copy-start.5
  13.2 0.1 bitcast_add_fusion
  13.4 0.0 copy-start
  13.4 0.0 copy-done.1
  13.4 0.1 fusion.8
  13.5 1.9 %collective-permute-start.1 = (f32[2,1,64,1024]{3,2,1,0:T(8,128)S(1)}, f32[2,1,64,1024]{3,2,1,0:T(8,128)S(1)}, u32[]{:S(2)}, u32[]{:S(2)}) collective-permute-start(f32[2,1,64,1024]{3,2,1,0:T(8,128)S(1)} %get-tuple-element.9), channel_id=1, source_target_pairs={{0,4},{4,8},{8,12},{12,16},{16,20},{20,24},{24,28},{28,32},{32,36}... | collective-permute-start | bytes 1572872 | tf_op jit(solution)/shard_map/ppermute | solution.py:21
  15.4 3.6 %collective-permute-start.2 = (f32[2,1,64,1024]{3,2,1,0:T(8,128)S(1)}, f32[2,1,64,1024]{3,2,1,0:T(8,128)S(1)}, u32[]{:S(2)}, u32[]{:S(2)}) collective-permute-start(f32[2,1,64,1024]{3,2,1,0:T(8,128)S(1)} %get-tuple-element.10), channel_id=1, source_target_pairs={{4,0},{8,4},{12,8},{16,12},{20,16},{24,20},{28,24},{32,28},{36,32}... | collective-permute-start | bytes 1572872 | tf_op jit(solution)/shard_map/ppermute | solution.py:22
  19.1 3.5 %collective-permute-start = (f32[2,2,1,1024]{3,2,1,0:T(1,128)S(1)}, f32[2,2,1,1024]{3,2,1,0:T(1,128)S(1)}, u32[]{:S(2)}, u32[]{:S(2)}) collective-permute-start(f32[2,2,1,1024]{3,2,1,0:T(1,128)S(1)} %get-tuple-element.11), channel_id=1, source_target_pairs={{0,1},{1,2},{2,3},{4,5},{5,6},{6,7},{8,9},{9,10},{10,11},{12,13},{... | collective-permute-start | bytes 49160 | tf_op jit(solution)/shard_map/ppermute | solution.py:21
  22.6 1.5 %collective-permute-start.3 = (f32[2,2,1,1024]{3,2,1,0:T(1,128)S(1)}, f32[2,2,1,1024]{3,2,1,0:T(1,128)S(1)}, u32[]{:S(2)}, u32[]{:S(2)}) collective-permute-start(f32[2,2,1,1024]{3,2,1,0:T(1,128)S(1)} %get-tuple-element.12), channel_id=1, source_target_pairs={{1,0},{2,1},{3,2},{5,4},{6,5},{7,6},{9,8},{10,9},{11,10},{13,12},{... | collective-permute-start | bytes 49160 | tf_op jit(solution)/shard_map/ppermute | solution.py:22
  24.1 0.0 copy-done.6
  24.1 0.1 copy.15
  24.2 0.1 broadcast_in_dim.16
  24.3 0.0 copy-done.5
  24.3 0.1 copy.14
  24.4 0.1 eq.15
  24.5 0.0 collective-permute-done
  24.5 3.7 %collective-permute-done.3 = f32[2,2,1,1024]{3,2,1,0:T(1,128)S(1)} collective-permute-done((f32[2,2,1,1024]{3,2,1,0:T(1,128)S(1)}, f32[2,2,1,1024]{3,2,1,0:T(1,128)S(1)}, u32[]{:S(2)}, u32[]{:S(2)}) %collective-permute-start.3) | collective-permute-done | bytes 16416 | tf_op jit(solution)/shard_map/ppermute | solution.py:22
  28.2 0.0 collective-permute-done.1
  28.2 0.0 collective-permute-done.2
  28.2 0.3 select_maximum_fusion
  28.6 0.0 copy-done
  28.6 0.2 slice_bitcast_fusion
  28.7 0.0 copy-start.4
  28.7 0.5 fusion.27
  29.2 0.6 copy-done.4
  29.8 0.8 fusion.13
  30.6 0.0 copy-start.2
  30.6 0.1 reshape.19
  30.7 5.4 %fusion.2 = f32[128,2048]{1,0:T(8,128)S(1)} fusion(f32[1024,128]{1,0:T(8,128)S(1)} %reshape.19, f32[1024]{0:T(1024)S(1)} %broadcast_in_dim.16, s32[1024]{0:T(1024)S(1)} %eq.15), kind=kOutput, calls=%fused_computation.2 | convolution fusion | flops 3225419776 | bytes 1581056 | tf_op jit(solution)/shard_map/dot_general | solution.py:72
  36.1 0.0 copy-done.2
  36.1 0.2 maximum_bitcast_fusion
  36.4 0.4 copy.19
  36.8 0.1 pad_slice_fusion
  36.9 2.5 %reshape.21 = f32[128,4095]{1,0:T(8,128)} reshape(f32[524160]{0:T(1024)S(1)} %pad_slice_fusion) | data formatting | bytes 4193280 | tf_op jit(solution)/shard_map/reshape | solution.py:77
  39.4 1.3 %slice_reduce_fusion = f32[2048]{0:T(1024)S(1)} fusion(f32[128,4095]{1,0:T(8,128)} %reshape.21), kind=kLoop, calls=%fused_computation.20 | loop fusion | flops 260096 | bytes 1056768 | tf_op jit(solution)/shard_map/reduce_sum | solution.py:78
  40.7 28.2 %all-gather = f32[16384]{0:T(1024)S(1)} all-gather(f32[2048]{0:T(1024)S(1)} %slice_reduce_fusion), channel_id=2, replica_groups=mesh['gz_0'=8,'gz_1'=4,'gz_2'=2,'gy'=4] {'gz_0'}, dimensions={0}, use_global_device_ids=true | all-gather | bytes 73728 | tf_op jit(solution)/shard_map/all_gather | solution.py:35
  68.9 12.0 %all-gather.1 = f32[8192]{0:T(1024)S(1)} all-gather(f32[2048]{0:T(1024)S(1)} %reduce_sum.55), channel_id=3, replica_groups=mesh['gz_0'=8,'gz_1'=4,'gz_2'=2,'gy'=4] {'gz_1'}, dimensions={0}, use_global_device_ids=true | all-gather | bytes 40960 | tf_op jit(solution)/shard_map/all_gather | solution.py:35
  80.9 1.8 %all-gather.2 = f32[4096]{0:T(1024)S(1)} all-gather(f32[2048]{0:T(1024)S(1)} %reduce_sum.56), channel_id=4, replica_groups=mesh['gz_0'=8,'gz_1'=4,'gz_2'=2,'gy'=4] {'gz_2'}, dimensions={0}, use_global_device_ids=true | all-gather | bytes 24576 | tf_op jit(solution)/shard_map/all_gather | solution.py:35
  82.8 12.2 %all-gather.3 = f32[8192]{0:T(1024)S(1)} all-gather(f32[2048]{0:T(1024)S(1)} %reduce_sum.57), channel_id=5, replica_groups=mesh['gz_0'=8,'gz_1'=4,'gz_2'=2,'gy'=4] {'gy'}, dimensions={0}, use_global_device_ids=true | all-gather | bytes 40960 | tf_op jit(solution)/shard_map/all_gather | solution.py:35
  95.0 0.6 multiply_reduce_fusion
  96.3 0.6 broadcast_divide_fusion
  (10 shorter events, 0.2 us)
Async XLA Ops:
  0.6 12.6 %copy-start.3 = (f32[2,64,1024]{2,1,0:T(8,128)S(1)}, f32[2,64,1024]{2,1,0:T(8,128)}, u32[]{:S(2)}) copy-start(f32[2,64,1024]{2,1,0:T(8,128)} %param.7) | copy-start | bytes 1572868
  0.6 12.7 %copy-start.1 = (f32[2,64,1024]{2,1,0:T(8,128)S(1)}, f32[2,64,1024]{2,1,0:T(8,128)}, u32[]{:S(2)}) copy-start(f32[2,64,1024]{2,1,0:T(8,128)} %param.11) | copy-start | bytes 1572868
  13.2 10.9 %copy-start.6 = (s32[2,64,8]{1,2,0:T(8,128)S(1)}, s32[2,64,8]{1,2,0:T(8,128)}, u32[]{:S(2)}) copy-start(s32[2,64,8]{1,2,0:T(8,128)} %param.13) | copy-start | bytes 12292
  13.2 11.1 %copy-start.5 = (s32[2,64,8]{1,2,0:T(8,128)S(1)}, s32[2,64,8]{1,2,0:T(8,128)}, u32[]{:S(2)}) copy-start(s32[2,64,8]{1,2,0:T(8,128)} %param.12) | copy-start | bytes 12292
  13.4 15.2 %copy-start = (f32[2,64,1024]{2,1,0:T(8,128)}, f32[2,64,1024]{2,1,0:T(8,128)S(1)}, u32[]{:S(2)}) copy-start(f32[2,64,1024]{2,1,0:T(8,128)S(1)} %bitcast_add_fusion) | copy-start | bytes 1572868
  13.5 14.7 %collective-permute-start.1 = (f32[2,1,64,1024]{3,2,1,0:T(8,128)S(1)}, f32[2,1,64,1024]{3,2,1,0:T(8,128)S(1)}, u32[]{:S(2)}, u32[]{:S(2)}) collective-permute-start(f32[2,1,64,1024]{3,2,1,0:T(8,128)S(1)} %get-tuple-element.9), channel_id=1, source_target_pairs={{0,4},{4,8},{8,12},{12,16},{16,20},{20,24},{24,28},{28,32},{32,36}... | collective-permute-start | bytes 1572872 | tf_op jit(solution)/shard_map/ppermute | solution.py:21
  15.4 12.8 %collective-permute-start.2 = (f32[2,1,64,1024]{3,2,1,0:T(8,128)S(1)}, f32[2,1,64,1024]{3,2,1,0:T(8,128)S(1)}, u32[]{:S(2)}, u32[]{:S(2)}) collective-permute-start(f32[2,1,64,1024]{3,2,1,0:T(8,128)S(1)} %get-tuple-element.10), channel_id=1, source_target_pairs={{4,0},{8,4},{12,8},{16,12},{20,16},{24,20},{28,24},{32,28},{36,32}... | collective-permute-start | bytes 1572872 | tf_op jit(solution)/shard_map/ppermute | solution.py:22
  19.1 5.4 %collective-permute-start = (f32[2,2,1,1024]{3,2,1,0:T(1,128)S(1)}, f32[2,2,1,1024]{3,2,1,0:T(1,128)S(1)}, u32[]{:S(2)}, u32[]{:S(2)}) collective-permute-start(f32[2,2,1,1024]{3,2,1,0:T(1,128)S(1)} %get-tuple-element.11), channel_id=1, source_target_pairs={{0,1},{1,2},{2,3},{4,5},{5,6},{6,7},{8,9},{9,10},{10,11},{12,13},{... | collective-permute-start | bytes 49160 | tf_op jit(solution)/shard_map/ppermute | solution.py:21
  22.6 5.6 %collective-permute-start.3 = (f32[2,2,1,1024]{3,2,1,0:T(1,128)S(1)}, f32[2,2,1,1024]{3,2,1,0:T(1,128)S(1)}, u32[]{:S(2)}, u32[]{:S(2)}) collective-permute-start(f32[2,2,1,1024]{3,2,1,0:T(1,128)S(1)} %get-tuple-element.12), channel_id=1, source_target_pairs={{1,0},{2,1},{3,2},{5,4},{6,5},{7,6},{9,8},{10,9},{11,10},{13,12},{... | collective-permute-start | bytes 49160 | tf_op jit(solution)/shard_map/ppermute | solution.py:22
  28.7 1.0 %copy-start.4 = (f32[2,64,1024]{2,1,0:T(8,128)S(1)}, f32[2,64,1024]{2,1,0:T(8,128)}, u32[]{:S(2)}) copy-start(f32[2,64,1024]{2,1,0:T(8,128)} %param.10) | copy-start | bytes 1572868
  30.6 5.6 %copy-start.2 = (f32[2,64,1024]{2,1,0:T(8,128)}, f32[2,64,1024]{2,1,0:T(8,128)S(1)}, u32[]{:S(2)}) copy-start(f32[2,64,1024]{2,1,0:T(8,128)S(1)} %fusion.13) | copy-start | bytes 1572868
